TPU v7x, 32 devices: a whole 2x2x4 slice. The times are simulated.
32 devices in a mesh: grp: 2 (over y), seq: 16 (over z, x, core).
Axes of the slice: x: 2, y: 2, z: 4, core: 2. Of those that a mesh axis runs over, the one named last changes fastest.
Arguments:
- frames: bfloat16 [4, 10240, 1280], P('grp', 'seq'), parts along dimension 0, may hold values from -120 to 120
- dec_states: bfloat16 [2, 256, 1280], P(None, 'grp'), parts along dimension 1, may hold values from -6 to 6
- w_query: bfloat16 [1280, 1280], P(None, 'seq'), may hold values from -0.15625 to 0.15625
- w_keyval: bfloat16 [1280, 2560], replicated, may hold values from -0.15625 to 0.15625
- w_output: bfloat16 [1280, 1280], P(None, 'seq'), may hold values from -0.15625 to 0.15625
- head_slope: float32 [20], replicated, may hold values from 0.3 to 12
- lengths: int32 [4, 16], P('grp'), parts along dimension 0, may hold values from 128 to 640, as said below
- positions: int32 [2, 256], P(None, 'grp'), parts along dimension 1, may hold values from 0 to 15
Outputs:
- attended: bfloat16 [2, 256, 1280], P(None, 'grp', 'seq'), parts along dimension 1
There are 2 independent parts, one for each index of `grp`. A program takes and returns all parts, laid end to end along the dimension named above; an argument that names none is the same for every part. Nothing has to cross between parts.
Inputs may be any that keep to these rules, and one draw needn't show every extreme that they name: `lengths`: every step has one block of exactly 640 valid frames.
All inputs are finite; a program needn't handle non-finite values.
Results may differ from a plain program's by a relative error of at most 0.005.
The roundings to bfloat16 on the way count: a program that leaves them out, or rounds other values in their place, can miss the bound.
Values may be sent and summed in bfloat16 or wider, within the bound.
A program may use at most 128 MiB of HBM per device.

v0:
```python
import functools
import math

import jax
import jax.numpy as jnp
from jax import lax
from jax.experimental import pallas as pl
from jax.experimental.pallas import tpu as pltpu
from jax.sharding import PartitionSpec as P

MESH = pl.DeviceIdType.MESH
EXTRA = 16
MASKED = -1e30


def rows_together(ref, first, count):
    parts = [ref[first + index].astype(jnp.float32) for index in range(count)]
    return jnp.concatenate(parts, axis=0)


def await_bytes(ref, count, sem):
    part = ref.at[pl.ds(0, count)]
    pltpu.make_async_copy(part, part, sem).wait()


def kernel(
    n,
    dec_ref,
    wq_ref,
    wout_ref,
    pos_ref,
    slope_ref,
    len_ref,
    frames_hbm,
    wkv_hbm,
    out_ref,
    frames_ref,
    wkv_ref,
    k_ref,
    vt_ref,
    q_ref,
    ctx_ref,
    stat_ref,
    got_ctx,
    got_stat,
    pair_ctx,
    pair_stat,
    sum_ctx,
    sum_stat,
    fin_ref,
    frame_sem,
    weight_sem,
    send_sem,
    recv_sem,
    hop_sem,
    pair_sem,
):
    me = lax.axis_index("seq")
    steps, frame_count, width = frames_hbm.shape
    tokens = dec_ref.shape[0]
    per_step = tokens // steps
    heads = k_ref.shape[0]
    size = width // heads
    rows = wq_ref.shape[0]
    groups = math.gcd(heads, n)
    group_chunks = n // groups
    group_heads = heads // groups
    tile = frames_ref.shape[1]
    half = wkv_ref.shape[2]
    tiles = frames_ref.shape[0]
    per_block = frame_count // tile
    scale = 1.0 / math.sqrt(size)

    def frame_copy(index):
        return pltpu.make_async_copy(
            frames_hbm.at[index // per_block, pl.ds((index % per_block) * tile, tile)],
            frames_ref.at[index],
            frame_sem.at[index],
        )

    def weight_copy(index):
        return pltpu.make_async_copy(
            wkv_hbm.at[:, pl.ds(pl.multiple_of(index * half, half), half)], wkv_ref.at[index], weight_sem.at[index]
        )

    frame_copy(0).start()
    weight_copy(0).start()
    for index in range(1, tiles):
        frame_copy(index).start()
    for index in range(1, wkv_ref.shape[0]):
        weight_copy(index).start()

    barrier = pltpu.get_barrier_semaphore()

    @pl.loop(1, n)
    def _(step):
        peer = lax.rem(me + step, n)
        pl.semaphore_signal(barrier, inc=1, device_id={"seq": peer}, device_id_type=MESH)

    own_query = lax.dot_general(
        wq_ref[...], dec_ref[...], (((1,), (1,)), ((), ())), preferred_element_type=jnp.float32
    )
    q_ref[me] = own_query.astype(jnp.bfloat16)
    pl.semaphore_wait(barrier, n - 1)

    def send(src, dst, sem, peer):
        pltpu.make_async_remote_copy(
            src_ref=src,
            dst_ref=dst,
            send_sem=send_sem.at[sem],
            recv_sem=recv_sem.at[sem],
            device_id={"seq": peer},
            device_id_type=MESH,
        ).start()

    partner = me + 1 - 2 * lax.rem(me, 2)
    chips = n // 2

    def pass_on(ref, chunk, sem):
        send(ref.at[chunk], ref.at[chunk], sem, partner)

    def hop(ref, step, sem, level):
        return pltpu.make_async_remote_copy(
            src_ref=ref.at[me],
            dst_ref=ref.at[me],
            send_sem=send_sem.at[sem],
            recv_sem=hop_sem.at[level, step],
            device_id={"seq": lax.rem(me + 2 * step, n)},
            device_id_type=MESH,
        )

    def spread(ref, sem, level):
        @pl.loop(1, chips)
        def _(step):
            hop(ref, step, sem, level).start()

        pass_on(ref, me, level)

    def relay(ref, sem, level):
        @pl.loop(1, chips)
        def _(step):
            hop(ref, step, sem, level).wait_recv()
            pass_on(ref, lax.rem(me - 2 * step + n, n), level)

    def settle(ref, sem, level):
        await_bytes(ref, chips - 1, send_sem.at[sem])
        await_bytes(ref, chips, recv_sem.at[level])
        await_bytes(ref, chips, send_sem.at[level])

    spread(q_ref, 2, 0)

    column = lax.broadcasted_iota(jnp.int32, (frame_count, size + EXTRA), 1)
    place = lax.broadcasted_iota(jnp.int32, (frame_count, size + EXTRA), 0)
    masks = []
    for older in range(steps):
        hidden = (place >= len_ref[older, me]) & (column == size)
        masks.append(jnp.where(hidden, MASKED, 0.0).astype(jnp.bfloat16))
    mask = jnp.concatenate(masks, axis=0)
    ones = jnp.ones((EXTRA, steps * frame_count), jnp.bfloat16)

    @pl.loop(0, heads)
    def _(head):
        k_ref[head] = mask
        vt_ref[head, size:, :] = ones

    parts = wkv_ref.shape[0] // 2
    part_heads = half // size

    def project(part, index):
        at = pl.ds(pl.multiple_of(index * tile, tile), tile)
        keyval = jnp.dot(frames_ref[index], wkv_ref[part], preferred_element_type=jnp.float32)
        return at, keyval.astype(jnp.bfloat16)

    for index in range(tiles):
        frame_copy(index).wait()

    @pl.loop(0, parts)
    def _(part):
        weight_copy(part).wait()
        for index in range(tiles):
            at, keyval = project(part, index)
            for local_head in range(part_heads):
                lanes = slice(local_head * size, (local_head + 1) * size)
                k_ref[part * part_heads + local_head, at, 0:size] = keyval[:, lanes]

    def project_values(part):
        weight_copy(parts + part).wait()
        for index in range(tiles):
            at, keyval = project(parts + part, index)
            turned = keyval.T
            for local_head in range(part_heads):
                lanes = slice(local_head * size, (local_head + 1) * size)
                vt_ref[part * part_heads + local_head, 0:size, at] = turned[lanes]

    pl.loop(0, parts - 2)(project_values)
    relay(q_ref, 2, 0)
    pl.loop(parts - 2, parts)(project_values)
    settle(q_ref, 2, 0)

    slot_place = lax.rem(me + 1, n).astype(jnp.float32)
    distance = jnp.abs(pos_ref[...].astype(jnp.float32) - slot_place) / n
    first_row = lax.broadcasted_iota(jnp.int32, (EXTRA, tokens), 0) == 0
    query_tail = jnp.where(first_row, 1.0, 0.0).astype(jnp.bfloat16)
    token_step = lax.broadcasted_iota(jnp.int32, (1, tokens), 1) // per_step

    row = lax.broadcasted_iota(jnp.int32, (rows, tokens), 0)

    def pass_sums(turn):
        group = lax.rem(me // group_chunks + 1 + turn, groups)
        await_bytes(pair_stat, group_chunks // 2, pair_sem.at[0, turn])
        await_bytes(pair_ctx, group_chunks // 2, pair_sem.at[1, turn])

        @pl.loop(0, group_chunks // 2)
        def _(index):
            chunk = group * group_chunks + 2 * index + lax.rem(me, 2)
            slot = chunk // 2
            one, two = stat_ref[chunk], pair_stat[slot]
            top = jnp.maximum(one[0:2], two[0:2])
            one_factor = jnp.exp(one[0:2] - top)
            two_factor = jnp.exp(two[0:2] - top)
            stat = jnp.concatenate([top, one[2:4] * one_factor + two[2:4] * two_factor], axis=0)
            is_one = row + lax.rem(chunk * rows, size) < size
            context = ctx_ref[chunk].astype(jnp.float32) * jnp.where(
                is_one, one_factor[0:1], one_factor[1:2]
            ) + pair_ctx[slot].astype(jnp.float32) * jnp.where(
                is_one, two_factor[0:1], two_factor[1:2]
            )
            context = context.astype(jnp.bfloat16)

            @pl.when(chunk != me)
            def _():
                sum_stat[slot] = stat
                sum_ctx[slot] = context
                send(sum_stat.at[slot], got_stat.at[me // 2], 4, chunk)
                send(sum_ctx.at[slot], got_ctx.at[me // 2], 5, chunk)

            @pl.when(chunk == me)
            def _():
                got_stat[slot] = stat
                got_ctx[slot] = context

    @pl.loop(0, groups)
    def _(turn):
        group = lax.rem(me // group_chunks + 1 + turn, groups)
        query_rows = rows_together(q_ref, group * group_chunks, group_chunks).astype(jnp.bfloat16)
        peaks, totals, contexts = [], [], []

        def scores(local_head):
            query = jnp.concatenate(
                [query_rows[local_head * size : (local_head + 1) * size], query_tail], axis=0
            )
            return [
                jnp.dot(
                    k_ref[
                        group * group_heads + local_head,
                        pl.ds(older * frame_count, frame_count),
                        :,
                    ],
                    query[:, older * per_step :],
                    preferred_element_type=jnp.float32,
                )
                for older in range(steps)
            ]

        ready = scores(0)
        for local_head in range(group_heads):
            head = group * group_heads + local_head
            raws = ready
            if local_head + 1 < group_heads:
                ready = scores(local_head + 1)
            slope = slope_ref[head]
            peak = context = None
            for older in range(steps):
                first = older * per_step
                block = pl.ds(older * frame_count, frame_count)
                raw = raws[older]
                raw_peak = jnp.max(raw, axis=0, keepdims=True)
                weights = jnp.exp2((raw - raw_peak) * (scale * math.log2(math.e)))
                part_context = jnp.dot(
                    vt_ref[head, :, block],
                    weights.astype(jnp.bfloat16),
                    preferred_element_type=jnp.float32,
                )
                age = (token_step[:, first:] - older).astype(jnp.float32)
                part_peak = raw_peak * scale - slope * (distance[:, first:] + age)
                if peak is None:
                    peak, context = part_peak, part_context
                    continue
                top = jnp.maximum(peak[:, first:], part_peak)
                old_factor = jnp.exp(peak[:, first:] - top)
                new_factor = jnp.exp(part_peak - top)
                merged = context[:, first:] * old_factor + part_context * new_factor
                peak = jnp.concatenate([peak[:, :first], top], axis=1)
                context = jnp.concatenate([context[:, :first], merged], axis=1)
            peaks.append(peak)
            totals.append(context[size : size + 1])
            contexts.append(context[:size])
        stacked = jnp.concatenate(contexts, axis=0)
        for index in range(group_chunks):
            low, high = index * rows, (index + 1) * rows
            one, two = low // size, (high - 1) // size
            chunk = group * group_chunks + index
            ctx_ref[chunk] = stacked[low:high].astype(jnp.bfloat16)
            stat_ref[chunk] = jnp.concatenate(
                [peaks[one], peaks[two], totals[one], totals[two]], axis=0
            )

        @pl.loop(0, group_chunks // 2)
        def _(index):
            chunk = group * group_chunks + 2 * index + 1 - lax.rem(me, 2)
            for kind, (src, dst) in enumerate(((stat_ref, pair_stat), (ctx_ref, pair_ctx))):
                pltpu.make_async_remote_copy(
                    src_ref=src.at[chunk],
                    dst_ref=dst.at[chunk // 2],
                    send_sem=send_sem.at[kind],
                    recv_sem=pair_sem.at[kind, turn],
                    device_id={"seq": partner},
                    device_id_type=MESH,
                ).start()

        @pl.when(turn > 0)
        def _():
            pass_sums(turn - 1)

    pass_sums(groups - 1)
    await_bytes(got_stat, chips - 1, recv_sem.at[4])
    await_bytes(got_ctx, chips - 1, recv_sem.at[5])
    await_bytes(sum_stat, chips - 1, send_sem.at[4])
    await_bytes(sum_ctx, chips - 1, send_sem.at[5])
    await_bytes(stat_ref, chips, send_sem.at[0])
    await_bytes(ctx_ref, chips, send_sem.at[1])

    top = lax.fori_loop(
        1, chips, lambda at, best: jnp.maximum(best, got_stat[at][0:2]), got_stat[0][0:2]
    )
    is_one = row + lax.rem(me * rows, size) < size

    def add(at, state):
        total, acc = state
        stat = got_stat[at]
        factor = jnp.exp(stat[0:2] - top)
        spread = jnp.where(is_one, factor[0:1], factor[1:2])
        return total + stat[2:4] * factor, acc + got_ctx[at].astype(jnp.float32) * spread

    total, acc = lax.fori_loop(
        0,
        chips,
        add,
        (jnp.zeros((2, tokens), jnp.float32), jnp.zeros((rows, tokens), jnp.float32)),
    )
    fin_ref[me] = (acc / jnp.where(is_one, total[0:1], total[1:2])).astype(jnp.bfloat16)

    spread(fin_ref, 3, 1)
    relay(fin_ref, 3, 1)
    settle(fin_ref, 3, 1)
    context = rows_together(fin_ref, 0, n).astype(jnp.bfloat16)
    attended = jnp.dot(wout_ref[...], context, preferred_element_type=jnp.float32)
    attended = attended.astype(jnp.bfloat16)
    for step in range(steps):
        out_ref[step] = attended[:, step * per_step : (step + 1) * per_step]


def local(n, frames, dec_states, w_query, w_keyval, w_output, head_slope, lengths, positions):
    steps, frame_count, width = frames.shape
    per_step = dec_states.shape[1]
    tokens = steps * per_step
    heads = head_slope.shape[0]
    size = width // heads
    rows = w_query.shape[1]
    keys = steps * frame_count
    tile = frame_count
    part = math.gcd(width, 256)
    vmem = pl.BlockSpec(memory_space=pltpu.VMEM)
    smem = pl.BlockSpec(memory_space=pltpu.SMEM)
    hbm = pl.BlockSpec(memory_space=pl.ANY)
    out = pl.pallas_call(
        functools.partial(kernel, n),
        out_shape=jax.ShapeDtypeStruct((steps, rows, per_step), jnp.bfloat16),
        in_specs=[vmem, vmem, vmem, vmem, smem, smem, hbm, hbm],
        out_specs=vmem,
        scratch_shapes=[
            pltpu.VMEM((keys // tile, tile, width), jnp.bfloat16),
            pltpu.VMEM((2 * width // part, width, part), jnp.bfloat16),
            pltpu.VMEM((heads, keys, size + EXTRA), jnp.bfloat16),
            pltpu.VMEM((heads, size + EXTRA, keys), jnp.bfloat16),
            pltpu.VMEM((n, rows, tokens), jnp.bfloat16),
            pltpu.VMEM((n, rows, tokens), jnp.bfloat16),
            pltpu.VMEM((n, 4, tokens), jnp.float32),
            pltpu.VMEM((n // 2, rows, tokens), jnp.bfloat16),
            pltpu.VMEM((n // 2, 4, tokens), jnp.float32),
            pltpu.VMEM((n // 2, rows, tokens), jnp.bfloat16),
            pltpu.VMEM((n // 2, 4, tokens), jnp.float32),
            pltpu.VMEM((n // 2, rows, tokens), jnp.bfloat16),
            pltpu.VMEM((n // 2, 4, tokens), jnp.float32),
            pltpu.VMEM((n, rows, tokens), jnp.bfloat16),
            pltpu.SemaphoreType.DMA((keys // tile,)),
            pltpu.SemaphoreType.DMA((2 * width // part,)),
            pltpu.SemaphoreType.DMA((6,)),
            pltpu.SemaphoreType.DMA((6,)),
            pltpu.SemaphoreType.DMA((2, n // 2)),
            pltpu.SemaphoreType.DMA((2, math.gcd(heads, n))),
        ],
        compiler_params=pltpu.CompilerParams(
            collective_id=0, has_side_effects=True, vmem_limit_bytes=60 * 1024 * 1024
        ),
    )(
        dec_states.reshape(tokens, width),
        w_query.T,
        w_output.T,
        positions.reshape(1, tokens),
        head_slope,
        lengths,
        frames,
        w_keyval,
    )
    return out.transpose(0, 2, 1)


def solution(mesh):
    return jax.shard_map(
        functools.partial(local, mesh.shape["seq"]),
        mesh=mesh,
        in_specs=(
            P("grp", "seq", None),
            P(None, "grp", None),
            P(None, "seq"),
            P(),
            P(None, "seq"),
            P(),
            P("grp", None),
            P(None, "grp"),
        ),
        out_specs=P(None, "grp", "seq"),
        check_vma=False,
    )
```

profile of v0, /device:TPU:25, one launch (start us, length us, event | category | flops | bytes accessed | tf_op | source)
XLA Modules:
  0.0 44.7 jit_solution(7980422389815314441)
XLA Ops:
  0.0 43.3 %shard_map.82 = bf16[2,80,128]{2,1,0:T(8,128)(2,1)} custom-call(bf16[256,1280]{1,0:T(8,128)(2,1)} %bitcast.5, bf16[80,1280]{1,0:T(8,128)(2,1)} %bitcast.6, bf16[80,1280]{1,0:T(8,128)(2,1)} %bitcast.7, s32[1,256]{1,0:T(1,128)} %bitcast.9, f32[20]{0:T(128)} %slope_ref.1, s32[2,16]{1,0:T(2,128)} %len_ref.1, bf16[2,640,1280]{2,1,0:T(8,128)(2,1)} %frames_hbm.1, ...), custom_call_target="tpu_custom_call" | custom-call | tf_op jit(solution)/shard_map/pallas_call | solution.py:376
  43.3 1.4 %copy.10 = bf16[2,128,80]{1,2,0:T(8,128)(2,1)} copy(bf16[2,128,80]{1,2,0:T(8,128)(2,1)} %bitcast.8) | data formatting | bytes 81920
where the time goes:
time: 44.9 us; the launch traced here: 44.7 us
  Pallas kernels  43.3 us (96%)
  local copies, waits for them, and re-layouts  1.4 us (3%)
    pallas_call x1, Pallas kernels, local(): pl.pallas_call(functools.partial(kernel, n), out_shape=jax.ShapeDtypeStru...  43.3 us
    unnamed x1, local copies, waits for them, and re-layouts  1.4 us

commit v1 on v0

--- a/solution.py
+++ b/solution.py
@@ -23,7 +23,7 @@
     pltpu.make_async_copy(part, part, sem).wait()
 
 
-def kernel(
+def plain_kernel(
     n,
     dec_ref,
     wq_ref,
@@ -360,7 +360,7 @@
         out_ref[step] = attended[:, step * per_step : (step + 1) * per_step]
 
 
-def local(n, frames, dec_states, w_query, w_keyval, w_output, head_slope, lengths, positions):
+def plain_local(n, frames, dec_states, w_query, w_keyval, w_output, head_slope, lengths, positions):
     steps, frame_count, width = frames.shape
     per_step = dec_states.shape[1]
     tokens = steps * per_step
@@ -374,7 +374,7 @@
     smem = pl.BlockSpec(memory_space=pltpu.SMEM)
     hbm = pl.BlockSpec(memory_space=pl.ANY)
     out = pl.pallas_call(
-        functools.partial(kernel, n),
+        functools.partial(plain_kernel, n),
         out_shape=jax.ShapeDtypeStruct((steps, rows, per_step), jnp.bfloat16),
         in_specs=[vmem, vmem, vmem, vmem, smem, smem, hbm, hbm],
         out_specs=vmem,
@@ -416,6 +416,607 @@
     return out.transpose(0, 2, 1)
 
 
+GROUPS = ((3, 2), (5, 2), (0, 2), (2, 1), (7, 1), (8, 1), (9, 1))
+PLAN = (
+    ("K1", "B0", "Q0", "V1", "K2", "V2", "Q1", "K3", "V3", "W0", "K0", "Y0", "A0", "V0", "M0", "A1", "W1", "K4")
+    + ("M1", "S0", "Y1", "A2", "S1", "A3", "M2", "C0", "A4", "M3", "V4", "S2", "M4", "C1", "A5", "X0", "A6", "M5")
+    + ("C3", "M6", "C4", "X1", "C2", "C5", "R0", "C6", "R3", "R1", "R4", "R2", "R5")
+)
+SUMS = ("near", "near", "near", "far", "far", "far", "far")
+SHARES = ("column", "column", "relay", "relay", "relay", "relay", "direct")
+
+
+def paired_kernel(
+    n,
+    pos_ref,
+    slope_ref,
+    len_ref,
+    dec_hbm,
+    wq_hbm,
+    wout_hbm,
+    frames_hbm,
+    wkv_hbm,
+    out_ref,
+    dec_ref,
+    wq_ref,
+    wout_ref,
+    frames_ref,
+    wkv_ref,
+    k_ref,
+    mask_ref,
+    vt_ref,
+    q_ref,
+    ctx_ref,
+    stat_ref,
+    pair_ctx,
+    pair_stat,
+    chip_ctx,
+    chip_stat,
+    got_ctx,
+    got_stat,
+    near_stat,
+    side_stat,
+    side_ctx,
+    fin_ref,
+    small_sem,
+    frame_sem,
+    weight_sem,
+    send_sem,
+    hop_sem,
+    relay_sem,
+    pair_sem,
+    got_sem,
+    near_sem,
+    fin_sem,
+    both_sem,
+    side_sem,
+):
+    me = lax.axis_index("seq")
+    core, chip = lax.rem(me, 2), me // 2
+    partner = me + 1 - 2 * core
+    chips = n // 2
+    steps, frame_count, width = frames_hbm.shape
+    tokens = dec_hbm.shape[0]
+    per_step = tokens // steps
+    pairs, lanes = vt_ref.shape[0], vt_ref.shape[1]
+    size = lanes // 2
+    rows = wq_hbm.shape[0]
+    half = wkv_ref.shape[2]
+    parts = wkv_ref.shape[0] // 2
+    part_pairs = half // lanes
+    scale = 1.0 / math.sqrt(size)
+    groups = GROUPS
+    side, level, levels = lax.rem(chip, 2), chip // 2, chips // 2
+
+    small = [
+        pltpu.make_async_copy(src, dst, small_sem.at[at])
+        for at, (src, dst) in enumerate(((dec_hbm, dec_ref), (wq_hbm, wq_ref), (wout_hbm, wout_ref)))
+    ]
+
+    def frame_copy(index):
+        return pltpu.make_async_copy(frames_hbm.at[index], frames_ref.at[index], frame_sem.at[index])
+
+    def weight_copy(index):
+        return pltpu.make_async_copy(
+            wkv_hbm.at[:, pl.ds(pl.multiple_of(index * half, half), half)], wkv_ref.at[index], weight_sem.at[index]
+        )
+
+    small[1].start()
+    small[0].start()
+    weight_order = [int(stage[1:]) + parts * (stage[0] == "V") for stage in PLAN if stage[0] in "KV"]
+    weight_copy(weight_order[0]).start(priority=1)
+    for step in range(steps):
+        frame_copy(step).start(priority=1)
+
+    barrier = pltpu.get_barrier_semaphore()
+
+    @pl.loop(1, n)
+    def _(step):
+        peer = lax.rem(me + step, n)
+        pl.semaphore_signal(barrier, inc=1, device_id={"seq": peer}, device_id_type=MESH)
+
+    def remote(src, dst, sent, got, peer):
+        return pltpu.make_async_remote_copy(
+            src_ref=src,
+            dst_ref=dst,
+            send_sem=sent,
+            recv_sem=got,
+            device_id={"seq": peer},
+            device_id_type=MESH,
+        )
+
+    def await_copy(ref, sem):
+        pltpu.make_async_copy(ref, ref, sem).wait()
+
+    def query_rows(device):
+        return q_ref.at[pl.ds(pl.multiple_of(device * rows, 16), rows)]
+
+    def await_small():
+        small[1].wait()
+        small[0].wait()
+
+    def project_query():
+        own_query = lax.dot_general(
+            wq_ref[...], dec_ref[...], (((1,), (1,)), ((), ())), preferred_element_type=jnp.float32
+        )
+        q_ref[pl.ds(pl.multiple_of(me * rows, 16), rows), :] = own_query.astype(jnp.bfloat16)
+
+    def await_barrier(_):
+        for index in weight_order[4:]:
+            weight_copy(index).start(priority=1)
+        small[2].start(priority=1)
+        pl.semaphore_wait(barrier, n - 1)
+
+    await_small()
+    project_query()
+
+    middle = chips // 4
+    wave_chips = (
+        list(range(middle, chips - middle)),
+        list(range(middle)) + list(range(chips - middle, chips)),
+    )
+    is_middle = (chip >= middle) & (chip < chips - middle)
+
+    def query_relay(device, wave):
+        block = query_rows(device)
+        remote(block, block, send_sem.at[1], relay_sem.at[wave], partner).start()
+
+    def spread_queries(wave):
+        @pl.when(is_middle if wave == 0 else jnp.logical_not(is_middle))
+        def _():
+            own = query_rows(me)
+
+            @pl.loop(1, chips)
+            def _(step):
+                remote(own, own, send_sem.at[0], hop_sem.at[chip], lax.rem(me + 2 * step, n)).start()
+
+            query_relay(me, wave)
+
+    def relay_queries(wave):
+        for source in wave_chips[wave]:
+
+            @pl.when(source != chip)
+            def _():
+                await_copy(query_rows(me), hop_sem.at[source])
+                query_relay(2 * source + core, wave)
+
+    def await_queries(wave):
+        await_copy(q_ref.at[pl.ds(0, rows * len(wave_chips[wave]))], relay_sem.at[wave])
+
+    place = lax.broadcasted_iota(jnp.int32, (frame_count, lanes), 0)
+    column = lax.broadcasted_iota(jnp.int32, (frame_count, lanes), 1)
+    for older in range(steps):
+        hidden = (place >= len_ref[older, me]) & (column == 0)
+        mask_ref[older * frame_count : (older + 1) * frame_count, :] = jnp.where(hidden, MASKED, 0.0).astype(
+            jnp.bfloat16
+        )
+
+    def project_keys(part):
+        weight_copy(part).wait()
+        for step in range(steps):
+            at = slice(step * frame_count, (step + 1) * frame_count)
+            keys = jnp.dot(frames_ref[step], wkv_ref[part], preferred_element_type=jnp.float32)
+            keys = keys.astype(jnp.bfloat16)
+            for index in range(part_pairs):
+                k_ref[part * part_pairs + index, at, :] = keys[:, index * lanes : (index + 1) * lanes]
+
+    def project_values(part):
+        weight_copy(parts + part).wait()
+        for step in range(steps):
+            at = slice(step * frame_count, (step + 1) * frame_count)
+            values = jnp.dot(frames_ref[step], wkv_ref[parts + part], preferred_element_type=jnp.float32)
+            turned = values.astype(jnp.bfloat16).T
+            for index in range(part_pairs):
+                vt_ref[part * part_pairs + index, :, at] = turned[index * lanes : (index + 1) * lanes]
+
+    def await_frames():
+        for step in range(steps):
+            frame_copy(step).wait()
+
+    for index in weight_order[1:4]:
+        weight_copy(index).start(priority=1)
+    await_frames()
+
+    slot_place = lax.rem(me + 1, n).astype(jnp.float32)
+    distance = jnp.abs(pos_ref[...].astype(jnp.float32) - slot_place) / n
+    tail_row = lax.broadcasted_iota(jnp.int32, (lanes, tokens), 0) == 0
+    tail = jnp.where(tail_row, 1.0, 0.0).astype(jnp.bfloat16)
+    blank = jnp.zeros((size, tokens), jnp.bfloat16)
+    ones = jnp.ones((EXTRA, frame_count), jnp.bfloat16)
+    first, second = slice(0, frame_count), slice(frame_count, 2 * frame_count)
+    early, late = slice(0, per_step), slice(per_step, tokens)
+
+    def attend_scores(pair):
+        query = q_ref[pl.ds(pl.multiple_of(pair * lanes, lanes), lanes), :]
+        one = jnp.concatenate([query[:size], blank, tail], axis=0)
+        two = jnp.concatenate([blank, query[size:], tail], axis=0)
+        both = jnp.concatenate([one[:, late], two[:, late]], axis=1)
+        old = jnp.concatenate([k_ref[pair, first, :], mask_ref[first, :]], axis=1)
+        new = jnp.concatenate([k_ref[pair, second, :], mask_ref[second, :]], axis=1)
+        return [
+            functools.partial(jnp.dot, keys, queries, preferred_element_type=jnp.float32)
+            for keys, queries in ((old, one), (old, two), (new, both))
+        ]
+
+    def soften(raw):
+        peak = jnp.max(raw, axis=0, keepdims=True)
+        weights = jnp.exp2((raw - peak) * (scale * math.log2(math.e)))
+        return peak * scale, weights.astype(jnp.bfloat16)
+
+    def attend_values(pair, kind):
+        if kind == 2:
+            stack = [vt_ref[pair, :, second], ones]
+        else:
+            stack = [vt_ref[pair, kind * size : (kind + 1) * size, first], ones]
+        return jnp.concatenate(stack, axis=0)
+
+    def attend(group):
+        first_pair, count = groups[group]
+        dots = []
+        for local_pair in range(count):
+            dots += [(local_pair, kind, call) for kind, call in enumerate(attend_scores(first_pair + local_pair))]
+        results = {}
+        ready = [dots[0][2](), dots[1][2]()]
+        for at, (local_pair, kind, _) in enumerate(dots):
+            raw = ready.pop(0)
+            if at + 2 < len(dots):
+                ready.append(dots[at + 2][2]())
+            peak, weights = soften(raw)
+            values = attend_values(first_pair + local_pair, kind)
+            results[local_pair, kind] = peak, jnp.dot(values, weights, preferred_element_type=jnp.float32)
+        peaks = [[], []]
+        totals = [[], []]
+        for local_pair in range(count):
+            pair = first_pair + local_pair
+            new_peaks, new_context = results[local_pair, 2]
+            for which in range(2):
+                slope = slope_ref[2 * pair + which]
+                at = pl.ds(pl.multiple_of(pair * lanes + which * size, size), size)
+                peak, context = results[local_pair, which]
+                peaks[0].append(peak[:, early] - slope * distance[:, early])
+                totals[0].append(context[size : size + 1, early])
+                ctx_ref[0, at, :] = context[:size, early].astype(jnp.bfloat16)
+                span = slice(which * per_step, (which + 1) * per_step)
+                old_peak = peak[:, late] - slope * (distance[:, late] + 1.0)
+                new_peak = new_peaks[:, span] - slope * distance[:, late]
+                top = jnp.maximum(old_peak, new_peak)
+                old_factor, new_factor = jnp.exp(old_peak - top), jnp.exp(new_peak - top)
+                own = slice(which * size, (which + 1) * size)
+                merged = context[:size, late] * old_factor + new_context[own, span] * new_factor
+                ctx_ref[1, at, :] = merged.astype(jnp.bfloat16)
+                peaks[1].append(top)
+                old_total = context[size : size + 1, late] * old_factor
+                totals[1].append(old_total + new_context[lanes : lanes + 1, span] * new_factor)
+        for step in range(2):
+            stat_ref[step, group, 0 : 4 * count, :] = jnp.concatenate(peaks[step] + totals[step], axis=0)
+        block = pl.ds(pl.multiple_of(first_pair * lanes, lanes), count * lanes)
+        other = 1 - core
+        remote(
+            stat_ref.at[other, group], pair_stat.at[group], send_sem.at[2], pair_sem.at[0, group], partner
+        ).start()
+        remote(
+            ctx_ref.at[other, block], pair_ctx.at[block], send_sem.at[3], pair_sem.at[1, group], partner
+        ).start()
+
+    def slices(first_pair, count):
+        part_rows = count * lanes // chips
+        base = first_pair * lanes
+
+        def block(owner):
+            place = lax.rem(owner, 2) * (chips // 2) + owner // 2
+            return pl.ds(pl.multiple_of(base + place * part_rows, 16), part_rows)
+
+        slot = pl.ds(pl.multiple_of(base // chips, 16), part_rows)
+        return part_rows, block, slot
+
+    def mix(one, two, heads):
+        top = jnp.maximum(one[:heads], two[:heads])
+        one_factor, two_factor = jnp.exp(one[:heads] - top), jnp.exp(two[:heads] - top)
+        total = one[heads : 2 * heads] * one_factor + two[heads : 2 * heads] * two_factor
+        return top, total, one_factor, two_factor
+
+    def merge_cores(group):
+        first_pair, count = groups[group]
+        part_rows, block, slot = slices(first_pair, count)
+        heads = 2 * count
+        await_copy(pair_stat.at[group], pair_sem.at[0, group])
+        await_copy(pair_ctx.at[pl.ds(0, count * lanes)], pair_sem.at[1, group])
+        top, total, one_factor, two_factor = mix(stat_ref[core, group], pair_stat[group], heads)
+        for head in range(heads):
+            at = slice(first_pair * lanes + head * size, first_pair * lanes + (head + 1) * size)
+            merged = (
+                ctx_ref[core, at, :].astype(jnp.float32) * one_factor[head : head + 1]
+                + pair_ctx[at, :].astype(jnp.float32) * two_factor[head : head + 1]
+            )
+            chip_ctx[at, :] = merged.astype(jnp.bfloat16)
+        if SUMS[group] == "near":
+            near_stat[group] = jnp.concatenate([top, total], axis=0)
+            block = side_rows(group, 1 - side)
+            peer = me + 2 - 4 * side
+            remote(
+                near_stat.at[group], side_stat.at[group], send_sem.at[12], near_sem.at[0, group], peer
+            ).start()
+            remote(
+                chip_ctx.at[block], side_ctx.at[block], send_sem.at[11], near_sem.at[1, group], peer
+            ).start()
+            return
+        for owner in range(chips):
+            head = (owner % 2 * levels + owner // 2) * part_rows // size
+            chip_stat[group, owner] = jnp.concatenate([top[head : head + 1], total[head : head + 1]], axis=0)
+
+        @pl.loop(1, chips)
+        def _(step):
+            owner = lax.rem(chip + step, chips)
+            peer = 2 * owner + core
+            remote(
+                chip_stat.at[group, owner], got_stat.at[group, chip], send_sem.at[4], got_sem.at[0, group], peer
+            ).start()
+            remote(
+                chip_ctx.at[block(owner)], got_ctx.at[chip, slot], send_sem.at[5], got_sem.at[1, group], peer
+            ).start()
+
+        got_stat[group, chip] = chip_stat[group, chip]
+        got_ctx[chip, slot, :] = chip_ctx[block(chip), :]
+
+    def side_rows(group, which):
+        first_pair, count = groups[group]
+        span = count * lanes // 2
+        return pl.ds(pl.multiple_of(first_pair * lanes + which * span, 16), span)
+
+    def merge_sides(group):
+        first_pair, count = groups[group]
+        part_rows, block, slot = slices(first_pair, count)
+        await_copy(side_stat.at[group], near_sem.at[0, group])
+        await_copy(side_ctx.at[pl.ds(0, count * lanes // 2)], near_sem.at[1, group])
+        stats = mix(near_stat[group], side_stat[group], 2 * count)
+        top, total, one_factor, two_factor = (
+            jnp.where(side == 0, stat[:count], stat[count:]) for stat in stats
+        )
+        base = first_pair * lanes + side * (count * lanes // 2)
+        for head in range(count):
+            at = pl.ds(pl.multiple_of(base + head * size, size), size)
+            merged = (
+                chip_ctx[at, :].astype(jnp.float32) * one_factor[head : head + 1]
+                + side_ctx[at, :].astype(jnp.float32) * two_factor[head : head + 1]
+            )
+            chip_ctx[at, :] = merged.astype(jnp.bfloat16)
+        for owner in range(levels):
+            head = owner * part_rows // size
+            chip_stat[group, owner] = jnp.concatenate([top[head : head + 1], total[head : head + 1]], axis=0)
+
+        @pl.loop(1, levels)
+        def _(step):
+            owner = lax.rem(level + step, levels)
+            peer = lax.rem(me + 4 * step, n)
+            remote(
+                chip_stat.at[group, owner], got_stat.at[group, level], send_sem.at[13], got_sem.at[0, group], peer
+            ).start()
+            remote(
+                chip_ctx.at[block(2 * owner + side)],
+                got_ctx.at[level, slot],
+                send_sem.at[10],
+                got_sem.at[1, group],
+                peer,
+            ).start()
+
+        got_stat[group, level] = chip_stat[group, level]
+        got_ctx[level, slot, :] = chip_ctx[block(chip), :]
+
+    def merge_chips(group):
+        first_pair, count = groups[group]
+        mode = SHARES[group]
+        sources = levels if SUMS[group] == "near" else chips
+        part_rows, block, slot = slices(first_pair, count)
+        await_copy(got_stat.at[group, pl.ds(0, sources - 1)], got_sem.at[0, group])
+        await_copy(got_ctx.at[pl.ds(0, sources - 1), pl.ds(0, part_rows)], got_sem.at[1, group])
+        stats = [got_stat[group, source] for source in range(sources)]
+        top = stats[0][0:1]
+        for stat in stats[1:]:
+            top = jnp.maximum(top, stat[0:1])
+        total = context = None
+        for source, stat in enumerate(stats):
+            factor = jnp.exp(stat[0:1] - top)
+            part_total = stat[1:2] * factor
+            part_context = got_ctx[source, slot, :].astype(jnp.float32) * factor
+            total = part_total if total is None else total + part_total
+            context = part_context if context is None else context + part_context
+        fin_ref[core, block(chip), :] = (context / total).astype(jnp.bfloat16)
+        own = fin_ref.at[core, block(chip)]
+        if mode == "direct":
+
+            @pl.loop(1, n)
+            def _(step):
+                remote(own, own, send_sem.at[7], fin_sem.at[group], lax.rem(me + step, n)).start()
+
+        else:
+            stride = 4 if mode == "column" else 2
+
+            @pl.loop(1, n // stride)
+            def _(step):
+                remote(
+                    own, own, send_sem.at[6], fin_sem.at[group], lax.rem(me + stride * step, n)
+                ).start()
+
+    def group_rows(group):
+        first_pair, count = groups[group]
+        return slice(first_pair * lanes, (first_pair + count) * lanes)
+
+    def await_slices(group, amount):
+        await_copy(fin_ref.at[0, pl.ds(0, amount * groups[group][1] * lanes // chips)], fin_sem.at[group])
+
+    def cross(group):
+        await_slices(group, levels - 1)
+        block = fin_ref.at[core, side_rows(group, side)]
+        remote(block, block, send_sem.at[9], side_sem.at[group], me + 2 - 4 * side).start()
+
+    def relay(group):
+        if SHARES[group] == "column":
+            await_copy(fin_ref.at[0, pl.ds(0, groups[group][1] * lanes // 2)], side_sem.at[group])
+        else:
+            await_slices(group, chips - 1)
+        block = fin_ref.at[core, group_rows(group)]
+        remote(block, block, send_sem.at[8], both_sem.at[group], partner).start()
+
+    stages = {
+        "K": project_keys,
+        "V": project_values,
+        "B": await_barrier,
+        "Q": spread_queries,
+        "W": relay_queries,
+        "Y": await_queries,
+        "A": attend,
+        "M": merge_cores,
+        "S": merge_sides,
+        "C": merge_chips,
+        "X": cross,
+        "R": relay,
+    }
+    for stage in PLAN:
+        stages[stage[0]](int(stage[1:]))
+
+    def await_both(group):
+        await_copy(fin_ref.at[0, group_rows(group)], both_sem.at[group])
+
+    small[2].wait()
+    direct = [group for group, mode in enumerate(SHARES) if mode == "direct"]
+    for group in range(direct[0]):
+        await_both(group)
+
+    def attended(begin, stop):
+        context = jnp.concatenate([fin_ref[0, begin:stop, :], fin_ref[1, begin:stop, :]], axis=1)
+        return jnp.dot(wout_ref[:, begin:stop], context, preferred_element_type=jnp.float32)
+
+    late_row = groups[direct[0]][0] * lanes
+    total = attended(0, late_row)
+    for group in direct:
+        await_slices(group, n - 1)
+    total = total + attended(late_row, width)
+    total = total.astype(jnp.bfloat16)
+    for step in range(steps):
+        out_ref[step] = total[:, step * per_step : (step + 1) * per_step]
+
+    def sent(amount, sem):
+        await_copy(fin_ref.at[0, pl.ds(0, amount)], send_sem.at[sem])
+
+    share_rows = {mode: 0 for mode in SHARES}
+    sum_rows = {mode: 0 for mode in SUMS}
+    sum_count = {mode: 0 for mode in SUMS}
+    for (_, count), shared, summed in zip(groups, SHARES, SUMS):
+        share_rows[shared] += count * lanes // chips
+        sum_rows[summed] += count * lanes // chips
+        sum_count[summed] += 1
+    await_copy(q_ref.at[pl.ds(0, rows * (chips - 1))], send_sem.at[0])
+    await_copy(q_ref.at[pl.ds(0, rows * chips)], send_sem.at[1])
+    await_copy(stat_ref.at[0], send_sem.at[2])
+    await_copy(ctx_ref.at[0], send_sem.at[3])
+    await_copy(got_stat.at[pl.ds(0, sum_count["far"]), pl.ds(0, chips - 1)], send_sem.at[4])
+    sent((chips - 1) * sum_rows["far"], 5)
+    sent((levels - 1) * share_rows["column"] + (chips - 1) * share_rows["relay"], 6)
+    sent((n - 1) * share_rows["direct"], 7)
+    sent(late_row, 8)
+    sent(levels * share_rows["column"], 9)
+    sent((levels - 1) * sum_rows["near"], 10)
+    sent(levels * sum_rows["near"], 11)
+    await_copy(side_stat.at[pl.ds(0, sum_count["near"])], send_sem.at[12])
+    await_copy(got_stat.at[pl.ds(0, sum_count["near"]), pl.ds(0, levels - 1)], send_sem.at[13])
+
+
+def paired_local(n, frames, dec_states, w_query, w_keyval, w_output, head_slope, lengths, positions):
+    steps, frame_count, width = frames.shape
+    per_step = dec_states.shape[1]
+    tokens = steps * per_step
+    heads = head_slope.shape[0]
+    lanes = 2 * (width // heads)
+    pairs = heads // 2
+    rows = w_query.shape[1]
+    keys = steps * frame_count
+    part = 2 * lanes
+    chips = n // 2
+    groups = len(GROUPS)
+    vmem = pl.BlockSpec(memory_space=pltpu.VMEM)
+    smem = pl.BlockSpec(memory_space=pltpu.SMEM)
+    hbm = pl.BlockSpec(memory_space=pl.ANY)
+    out = pl.pallas_call(
+        functools.partial(paired_kernel, n),
+        out_shape=jax.ShapeDtypeStruct((steps, rows, per_step), jnp.bfloat16),
+        in_specs=[vmem, smem, smem, hbm, hbm, hbm, hbm, hbm],
+        out_specs=vmem,
+        scratch_shapes=[
+            pltpu.VMEM((tokens, width), jnp.bfloat16),
+            pltpu.VMEM((rows, width), jnp.bfloat16),
+            pltpu.VMEM((rows, width), jnp.bfloat16),
+            pltpu.VMEM((steps, frame_count, width), jnp.bfloat16),
+            pltpu.VMEM((2 * width // part, width, part), jnp.bfloat16),
+            pltpu.VMEM((pairs, keys, lanes), jnp.bfloat16),
+            pltpu.VMEM((keys, lanes), jnp.bfloat16),
+            pltpu.VMEM((pairs, lanes, keys), jnp.bfloat16),
+            pltpu.VMEM((width, tokens), jnp.bfloat16),
+            pltpu.VMEM((2, width, per_step), jnp.bfloat16),
+            pltpu.VMEM((2, groups, 8, per_step), jnp.float32),
+            pltpu.VMEM((width, per_step), jnp.bfloat16),
+            pltpu.VMEM((groups, 8, per_step), jnp.float32),
+            pltpu.VMEM((width, per_step), jnp.bfloat16),
+            pltpu.VMEM((groups, chips, 2, per_step), jnp.float32),
+            pltpu.VMEM((chips, width // chips, per_step), jnp.bfloat16),
+            pltpu.VMEM((groups, chips, 2, per_step), jnp.float32),
+            pltpu.VMEM((groups, 8, per_step), jnp.float32),
+            pltpu.VMEM((groups, 8, per_step), jnp.float32),
+            pltpu.VMEM((width, per_step), jnp.bfloat16),
+            pltpu.VMEM((2, width, per_step), jnp.bfloat16),
+            pltpu.SemaphoreType.DMA((3,)),
+            pltpu.SemaphoreType.DMA((steps,)),
+            pltpu.SemaphoreType.DMA((2 * width // part,)),
+            pltpu.SemaphoreType.DMA((14,)),
+            pltpu.SemaphoreType.DMA((chips,)),
+            pltpu.SemaphoreType.DMA((2,)),
+            pltpu.SemaphoreType.DMA((2, groups)),
+            pltpu.SemaphoreType.DMA((2, groups)),
+            pltpu.SemaphoreType.DMA((2, groups)),
+            pltpu.SemaphoreType.DMA((groups,)),
+            pltpu.SemaphoreType.DMA((groups,)),
+            pltpu.SemaphoreType.DMA((groups,)),
+        ],
+        compiler_params=pltpu.CompilerParams(
+            collective_id=0, has_side_effects=True, vmem_limit_bytes=60 * 1024 * 1024
+        ),
+    )(
+        positions.reshape(1, tokens),
+        head_slope,
+        lengths,
+        dec_states.reshape(tokens, width),
+        w_query.T,
+        w_output.T,
+        frames,
+        w_keyval,
+    )
+    return out.transpose(0, 2, 1)
+
+
+def fits_pairs(n, frames, dec_states, w_query, head_slope):
+    steps, frame_count, width = frames.shape
+    per_step, heads = dec_states.shape[1], head_slope.shape[0]
+    size = width // heads
+    chips = n // 2
+    return (
+        steps == 2
+        and n % 4 == 0
+        and heads % 4 == 0
+        and heads // 2 == sum(count for _, count in GROUPS)
+        and n % 8 == 0
+        and size == 64
+        and per_step == 2 * size
+        and frame_count % 128 == 0
+        and w_query.shape[1] % 16 == 0
+        and (2 * size) % (16 * chips) == 0
+    )
+
+
+def local(n, frames, dec_states, w_query, w_keyval, w_output, head_slope, lengths, positions):
+    paired = fits_pairs(n, frames, dec_states, w_query, head_slope)
+    run = paired_local if paired else plain_local
+    return run(n, frames, dec_states, w_query, w_keyval, w_output, head_slope, lengths, positions)
+
+
 def solution(mesh):
     return jax.shard_map(
         functools.partial(local, mesh.shape["seq"]),

time: 44.9 us -> 42.4 us (0.944)
  the two profiles are of different devices: /device:TPU:25 before, /device:TPU:1 now
where the time goes in v1:
time: 42.4 us; the launch traced here: 41.8 us
  Pallas kernels  40.4 us (95%)
  local copies, waits for them, and re-layouts  1.4 us (3%)
    pallas_call x1, Pallas kernels, paired_local(): pl.pallas_call(functools.partial(paired_kernel, n), out_shape=jax.ShapeDt...  40.4 us
    unnamed x1, local copies, waits for them, and re-layouts  1.4 us

profile of v1, /device:TPU:1, one launch (start us, length us, event | category | flops | bytes accessed | tf_op | source)
XLA Modules:
  0.0 41.8 jit_solution(13302206056529592486)
XLA Ops:
  0.0 40.4 %shard_map.82 = bf16[2,80,128]{2,1,0:T(8,128)(2,1)} custom-call(s32[1,256]{1,0:T(1,128)} %bitcast.9, f32[20]{0:T(128)} %slope_ref.1, s32[2,16]{1,0:T(2,128)} %len_ref.1, bf16[256,1280]{1,0:T(8,128)(2,1)} %bitcast.5, bf16[80,1280]{1,0:T(8,128)(2,1)} %bitcast.6, bf16[80,1280]{1,0:T(8,128)(2,1)} %bitcast.7, bf16[2,640,1280]{2,1,0:T(8,128)(2,1)} %frames_hbm.1, ...), custom_call_target="tpu_custom_call" | custom-call | tf_op jit(solution)/shard_map/pallas_call | solution.py:939
  40.4 1.4 %copy.10 = bf16[2,128,80]{1,2,0:T(8,128)(2,1)} copy(bf16[2,128,80]{1,2,0:T(8,128)(2,1)} %bitcast.8) | data formatting | bytes 81920

commit v2 on v1

--- a/solution.py
+++ b/solution.py
@@ -418,25 +418,29 @@
 
 GROUPS = ((3, 2), (5, 2), (0, 2), (2, 1), (7, 1), (8, 1), (9, 1))
 PLAN = (
-    ("K1", "B0", "Q0", "V1", "K2", "V2", "Q1", "K3", "V3", "W0", "K0", "Y0", "A0", "V0", "M0", "A1", "W1", "K4")
-    + ("M1", "S0", "Y1", "A2", "S1", "A3", "M2", "C0", "A4", "M3", "V4", "S2", "M4", "C1", "A5", "X0", "A6", "M5")
-    + ("C3", "M6", "C4", "X1", "C2", "C5", "R0", "C6", "R3", "R1", "R4", "R2", "R5")
+    ("K1", "B0", "Q0", "V1", "K2", "V2", "K3", "Q1", "V3", "W0", "K0", "Y0", "A0", "A1", "M0", "W1", "K4", "M1")
+    + ("Y1", "A2", "A3", "M2", "C0", "A4", "M3", "C1", "A5", "M4", "A6", "M5", "M6", "C2", "X0", "C3", "X1", "C4")
+    + ("R0", "C5", "C6", "R1", "R2", "R3", "R4", "R5")
 )
-SUMS = ("near", "near", "near", "far", "far", "far", "far")
+BESIDE = {0: "V0", 2: "V4"}
+SUMS = ("far", "far", "far", "far", "far", "far", "far")
 SHARES = ("column", "column", "relay", "relay", "relay", "relay", "direct")
 
 
 def paired_kernel(
     n,
-    pos_ref,
-    slope_ref,
-    len_ref,
+    pos_hbm,
+    slope_hbm,
+    len_hbm,
     dec_hbm,
     wq_hbm,
     wout_hbm,
     frames_hbm,
     wkv_hbm,
     out_ref,
+    pos_ref,
+    slope_ref,
+    len_ref,
     dec_ref,
     wq_ref,
     wout_ref,
@@ -490,7 +494,16 @@
 
     small = [
         pltpu.make_async_copy(src, dst, small_sem.at[at])
-        for at, (src, dst) in enumerate(((dec_hbm, dec_ref), (wq_hbm, wq_ref), (wout_hbm, wout_ref)))
+        for at, (src, dst) in enumerate(
+            (
+                (dec_hbm, dec_ref),
+                (wq_hbm, wq_ref),
+                (wout_hbm, wout_ref),
+                (pos_hbm, pos_ref),
+                (slope_hbm, slope_ref),
+                (len_hbm, len_ref),
+            )
+        )
     ]
 
     def frame_copy(index):
@@ -501,9 +514,10 @@
             wkv_hbm.at[:, pl.ds(pl.multiple_of(index * half, half), half)], wkv_ref.at[index], weight_sem.at[index]
         )
 
-    small[1].start()
-    small[0].start()
-    weight_order = [int(stage[1:]) + parts * (stage[0] == "V") for stage in PLAN if stage[0] in "KV"]
+    for at in (1, 0, 5, 4, 3):
+        small[at].start()
+    ordered = [stage if stage[0] in "KV" else BESIDE.get(int(stage[1:]), "B") for stage in PLAN if stage[0] in "KVA"]
+    weight_order = [int(stage[1:]) + parts * (stage[0] == "V") for stage in ordered if stage != "B"]
     weight_copy(weight_order[0]).start(priority=1)
     for step in range(steps):
         frame_copy(step).start(priority=1)
@@ -532,8 +546,8 @@
         return q_ref.at[pl.ds(pl.multiple_of(device * rows, 16), rows)]
 
     def await_small():
-        small[1].wait()
-        small[0].wait()
+        for at in (1, 0, 5, 4, 3):
+            small[at].wait()
 
     def project_query():
         own_query = lax.dot_general(
@@ -591,23 +605,40 @@
             jnp.bfloat16
         )
 
+    def keys_piece(part, step, begin, stop):
+        keys = jnp.dot(
+            frames_ref[step, begin:stop, :], wkv_ref[part], preferred_element_type=jnp.float32
+        ).astype(jnp.bfloat16)
+        at = slice(step * frame_count + begin, step * frame_count + stop)
+        for index in range(part_pairs):
+            k_ref[part * part_pairs + index, at, :] = keys[:, index * lanes : (index + 1) * lanes]
+
+    def values_piece(part, step, begin, stop):
+        values = jnp.dot(
+            frames_ref[step, begin:stop, :], wkv_ref[parts + part], preferred_element_type=jnp.float32
+        )
+        turned = values.astype(jnp.bfloat16).T
+        at = slice(step * frame_count + begin, step * frame_count + stop)
+        for index in range(part_pairs):
+            vt_ref[part * part_pairs + index, :, at] = turned[index * lanes : (index + 1) * lanes]
+
+    def project(kind, part, cuts):
+        piece = keys_piece if kind == "K" else values_piece
+        return [
+            functools.partial(piece, part, step, begin, stop)
+            for step in range(steps)
+            for begin, stop in zip(cuts, cuts[1:])
+        ]
+
     def project_keys(part):
         weight_copy(part).wait()
-        for step in range(steps):
-            at = slice(step * frame_count, (step + 1) * frame_count)
-            keys = jnp.dot(frames_ref[step], wkv_ref[part], preferred_element_type=jnp.float32)
-            keys = keys.astype(jnp.bfloat16)
-            for index in range(part_pairs):
-                k_ref[part * part_pairs + index, at, :] = keys[:, index * lanes : (index + 1) * lanes]
+        for piece in project("K", part, (0, frame_count)):
+            piece()
 
     def project_values(part):
         weight_copy(parts + part).wait()
-        for step in range(steps):
-            at = slice(step * frame_count, (step + 1) * frame_count)
-            values = jnp.dot(frames_ref[step], wkv_ref[parts + part], preferred_element_type=jnp.float32)
-            turned = values.astype(jnp.bfloat16).T
-            for index in range(part_pairs):
-                vt_ref[part * part_pairs + index, :, at] = turned[index * lanes : (index + 1) * lanes]
+        for piece in project("V", part, (0, frame_count)):
+            piece()
 
     def await_frames():
         for step in range(steps):
@@ -652,6 +683,12 @@
 
     def attend(group):
         first_pair, count = groups[group]
+        beside = []
+        if group in BESIDE:
+            kind, part = BESIDE[group][0], int(BESIDE[group][1:])
+            weight_copy(part + parts * (kind == "V")).wait()
+            half_frames = frame_count // 256 * 128
+            beside = project(kind, part, (0, half_frames, frame_count))
         dots = []
         for local_pair in range(count):
             dots += [(local_pair, kind, call) for kind, call in enumerate(attend_scores(first_pair + local_pair))]
@@ -661,9 +698,13 @@
             raw = ready.pop(0)
             if at + 2 < len(dots):
                 ready.append(dots[at + 2][2]())
+            if beside:
+                beside.pop(0)()
             peak, weights = soften(raw)
             values = attend_values(first_pair + local_pair, kind)
             results[local_pair, kind] = peak, jnp.dot(values, weights, preferred_element_type=jnp.float32)
+        for piece in beside:
+            piece()
         peaks = [[], []]
         totals = [[], []]
         for local_pair in range(count):
@@ -915,10 +956,11 @@
     sent((n - 1) * share_rows["direct"], 7)
     sent(late_row, 8)
     sent(levels * share_rows["column"], 9)
-    sent((levels - 1) * sum_rows["near"], 10)
-    sent(levels * sum_rows["near"], 11)
-    await_copy(side_stat.at[pl.ds(0, sum_count["near"])], send_sem.at[12])
-    await_copy(got_stat.at[pl.ds(0, sum_count["near"]), pl.ds(0, levels - 1)], send_sem.at[13])
+    if "near" in SUMS:
+        sent((levels - 1) * sum_rows["near"], 10)
+        sent(levels * sum_rows["near"], 11)
+        await_copy(side_stat.at[pl.ds(0, sum_count["near"])], send_sem.at[12])
+        await_copy(got_stat.at[pl.ds(0, sum_count["near"]), pl.ds(0, levels - 1)], send_sem.at[13])
 
 
 def paired_local(n, frames, dec_states, w_query, w_keyval, w_output, head_slope, lengths, positions):
@@ -934,14 +976,16 @@
     chips = n // 2
     groups = len(GROUPS)
     vmem = pl.BlockSpec(memory_space=pltpu.VMEM)
-    smem = pl.BlockSpec(memory_space=pltpu.SMEM)
-    hbm = pl.BlockSpec(memory_space=pl.ANY)
+    hbm = pl.BlockSpec(memory_space=pltpu.HBM)
     out = pl.pallas_call(
         functools.partial(paired_kernel, n),
-        out_shape=jax.ShapeDtypeStruct((steps, rows, per_step), jnp.bfloat16),
-        in_specs=[vmem, smem, smem, hbm, hbm, hbm, hbm, hbm],
+        out_shape=pltpu.VMEM((steps, rows, per_step), jnp.bfloat16),
+        in_specs=[hbm] * 8,
         out_specs=vmem,
         scratch_shapes=[
+            pltpu.VMEM((1, tokens), jnp.int32),
+            pltpu.SMEM((heads,), jnp.float32),
+            pltpu.SMEM(lengths.shape, jnp.int32),
             pltpu.VMEM((tokens, width), jnp.bfloat16),
             pltpu.VMEM((rows, width), jnp.bfloat16),
             pltpu.VMEM((rows, width), jnp.bfloat16),
@@ -963,7 +1007,7 @@
             pltpu.VMEM((groups, 8, per_step), jnp.float32),
             pltpu.VMEM((width, per_step), jnp.bfloat16),
             pltpu.VMEM((2, width, per_step), jnp.bfloat16),
-            pltpu.SemaphoreType.DMA((3,)),
+            pltpu.SemaphoreType.DMA((6,)),
             pltpu.SemaphoreType.DMA((steps,)),
             pltpu.SemaphoreType.DMA((2 * width // part,)),
             pltpu.SemaphoreType.DMA((14,)),
@@ -977,17 +1021,22 @@
             pltpu.SemaphoreType.DMA((groups,)),
         ],
         compiler_params=pltpu.CompilerParams(
-            collective_id=0, has_side_effects=True, vmem_limit_bytes=60 * 1024 * 1024
+            collective_id=0, has_side_effects=True, vmem_limit_bytes=40 * 1024 * 1024
         ),
     )(
-        positions.reshape(1, tokens),
-        head_slope,
-        lengths,
-        dec_states.reshape(tokens, width),
-        w_query.T,
-        w_output.T,
-        frames,
-        w_keyval,
+        *(
+            pltpu.with_memory_space_constraint(value, pltpu.HBM)
+            for value in (
+                positions.reshape(1, tokens),
+                head_slope,
+                lengths,
+                dec_states.reshape(tokens, width),
+                w_query.T,
+                w_output.T,
+                frames,
+                w_keyval,
+            )
+        )
     )
     return out.transpose(0, 2, 1)
 

time: 42.4 us -> 38.7 us (0.913)
  Pallas kernels: 40.4 us -> 37.9 us
  local copies, waits for them, and re-layouts: 1.4 us -> 0.62 us
    pallas_call x1, Pallas kernels: 40.4 us -> 37.9 us  [paired_local(): pl.pallas_call(functools.partial(paired_kernel, n), out_shape=pltpu.VMEM(...]
    unnamed x1, local copies, waits for them, and re-layouts: 1.4 us -> 0.62 us
where the time goes in v2:
time: 38.7 us; the launch traced here: 38.5 us
  Pallas kernels  37.9 us (98%)
  local copies, waits for them, and re-layouts  0.62 us (2%)
    pallas_call x1, Pallas kernels, paired_local(): pl.pallas_call(functools.partial(paired_kernel, n), out_shape=pltpu.VMEM(...  37.9 us

profile of v2, /device:TPU:1, one launch (start us, length us, event | category | flops | bytes accessed | tf_op | source)
XLA Modules:
  0.0 38.5 jit_solution(5234531355274479018)
XLA Ops:
  0.0 37.9 %shard_map.82 = bf16[2,80,128]{2,1,0:T(8,128)(2,1)S(1)} custom-call(s32[1,256]{1,0:T(1,128)} %bitcast.9, f32[20]{0:T(128)} %slope_hbm.1, s32[2,16]{1,0:T(2,128)} %len_hbm.1, bf16[256,1280]{1,0:T(8,128)(2,1)} %bitcast.6, bf16[80,1280]{1,0:T(8,128)(2,1)} %bitcast.7, bf16[80,1280]{1,0:T(8,128)(2,1)} %bitcast.8, bf16[2,640,1280]{2,1,0:T(8,128)(2,1)} %frames_hbm.1, ...), custom_call_target="tpu_custom_call" | custom-call | tf_op jit(solution)/shard_map/pallas_call | solution.py:980
  37.9 0.6 %copy.10 = bf16[2,128,80]{1,2,0:T(8,128)(2,1)} copy(bf16[2,128,80]{1,2,0:T(8,128)(2,1)S(1)} %bitcast.5) | data formatting | bytes 81920

commit v3 on v2

--- a/solution.py
+++ b/solution.py
@@ -423,7 +423,6 @@
     + ("R0", "C5", "C6", "R1", "R2", "R3", "R4", "R5")
 )
 BESIDE = {0: "V0", 2: "V4"}
-SUMS = ("far", "far", "far", "far", "far", "far", "far")
 SHARES = ("column", "column", "relay", "relay", "relay", "relay", "direct")
 
 
@@ -458,9 +457,6 @@
     chip_stat,
     got_ctx,
     got_stat,
-    near_stat,
-    side_stat,
-    side_ctx,
     fin_ref,
     small_sem,
     frame_sem,
@@ -470,7 +466,6 @@
     relay_sem,
     pair_sem,
     got_sem,
-    near_sem,
     fin_sem,
     both_sem,
     side_sem,
@@ -490,7 +485,8 @@
     part_pairs = half // lanes
     scale = 1.0 / math.sqrt(size)
     groups = GROUPS
-    side, level, levels = lax.rem(chip, 2), chip // 2, chips // 2
+    side, levels = lax.rem(chip, 2), chips // 2
+    owners = list(range(chips // 4, chips - chips // 4))
 
     small = [
         pltpu.make_async_copy(src, dst, small_sem.at[at])
@@ -740,15 +736,17 @@
         ).start()
 
     def slices(first_pair, count):
-        part_rows = count * lanes // chips
+        part_rows = count * lanes // len(owners)
         base = first_pair * lanes
 
+        def place(owner):
+            return owner % 2 * (levels // 2) + owner // 2 - levels // 4
+
         def block(owner):
-            place = lax.rem(owner, 2) * (chips // 2) + owner // 2
-            return pl.ds(pl.multiple_of(base + place * part_rows, 16), part_rows)
-
-        slot = pl.ds(pl.multiple_of(base // chips, 16), part_rows)
-        return part_rows, block, slot
+            return pl.ds(pl.multiple_of(base + place(owner) * part_rows, 16), part_rows)
+
+        slot = pl.ds(pl.multiple_of(base // len(owners), 16), part_rows)
+        return part_rows, place, block, slot
 
     def mix(one, two, heads):
         top = jnp.maximum(one[:heads], two[:heads])
@@ -758,7 +756,7 @@
 
     def merge_cores(group):
         first_pair, count = groups[group]
-        part_rows, block, slot = slices(first_pair, count)
+        part_rows, place, block, slot = slices(first_pair, count)
         heads = 2 * count
         await_copy(pair_stat.at[group], pair_sem.at[0, group])
         await_copy(pair_ctx.at[pl.ds(0, count * lanes)], pair_sem.at[1, group])
@@ -770,87 +768,39 @@
                 + pair_ctx[at, :].astype(jnp.float32) * two_factor[head : head + 1]
             )
             chip_ctx[at, :] = merged.astype(jnp.bfloat16)
-        if SUMS[group] == "near":
-            near_stat[group] = jnp.concatenate([top, total], axis=0)
-            block = side_rows(group, 1 - side)
-            peer = me + 2 - 4 * side
-            remote(
-                near_stat.at[group], side_stat.at[group], send_sem.at[12], near_sem.at[0, group], peer
-            ).start()
-            remote(
-                chip_ctx.at[block], side_ctx.at[block], send_sem.at[11], near_sem.at[1, group], peer
-            ).start()
-            return
-        for owner in range(chips):
-            head = (owner % 2 * levels + owner // 2) * part_rows // size
+        for owner in owners:
+            head = place(owner) * part_rows // size
             chip_stat[group, owner] = jnp.concatenate([top[head : head + 1], total[head : head + 1]], axis=0)
 
-        @pl.loop(1, chips)
-        def _(step):
-            owner = lax.rem(chip + step, chips)
-            peer = 2 * owner + core
-            remote(
-                chip_stat.at[group, owner], got_stat.at[group, chip], send_sem.at[4], got_sem.at[0, group], peer
-            ).start()
-            remote(
-                chip_ctx.at[block(owner)], got_ctx.at[chip, slot], send_sem.at[5], got_sem.at[1, group], peer
-            ).start()
-
-        got_stat[group, chip] = chip_stat[group, chip]
-        got_ctx[chip, slot, :] = chip_ctx[block(chip), :]
-
-    def side_rows(group, which):
-        first_pair, count = groups[group]
-        span = count * lanes // 2
-        return pl.ds(pl.multiple_of(first_pair * lanes + which * span, 16), span)
-
-    def merge_sides(group):
-        first_pair, count = groups[group]
-        part_rows, block, slot = slices(first_pair, count)
-        await_copy(side_stat.at[group], near_sem.at[0, group])
-        await_copy(side_ctx.at[pl.ds(0, count * lanes // 2)], near_sem.at[1, group])
-        stats = mix(near_stat[group], side_stat[group], 2 * count)
-        top, total, one_factor, two_factor = (
-            jnp.where(side == 0, stat[:count], stat[count:]) for stat in stats
-        )
-        base = first_pair * lanes + side * (count * lanes // 2)
-        for head in range(count):
-            at = pl.ds(pl.multiple_of(base + head * size, size), size)
-            merged = (
-                chip_ctx[at, :].astype(jnp.float32) * one_factor[head : head + 1]
-                + side_ctx[at, :].astype(jnp.float32) * two_factor[head : head + 1]
-            )
-            chip_ctx[at, :] = merged.astype(jnp.bfloat16)
-        for owner in range(levels):
-            head = owner * part_rows // size
-            chip_stat[group, owner] = jnp.concatenate([top[head : head + 1], total[head : head + 1]], axis=0)
-
-        @pl.loop(1, levels)
-        def _(step):
-            owner = lax.rem(level + step, levels)
-            peer = lax.rem(me + 4 * step, n)
-            remote(
-                chip_stat.at[group, owner], got_stat.at[group, level], send_sem.at[13], got_sem.at[0, group], peer
-            ).start()
-            remote(
-                chip_ctx.at[block(2 * owner + side)],
-                got_ctx.at[level, slot],
-                send_sem.at[10],
-                got_sem.at[1, group],
-                peer,
-            ).start()
-
-        got_stat[group, level] = chip_stat[group, level]
-        got_ctx[level, slot, :] = chip_ctx[block(chip), :]
+            @pl.when(owner != chip)
+            def _():
+                peer = 2 * owner + core
+                remote(
+                    chip_stat.at[group, owner],
+                    got_stat.at[group, chip],
+                    send_sem.at[4],
+                    got_sem.at[0, group],
+                    peer,
+                ).start()
+                remote(
+                    chip_ctx.at[block(owner)], got_ctx.at[chip, slot], send_sem.at[5], got_sem.at[1, group], peer
+                ).start()
+
+        @pl.when(is_middle)
+        def _():
+            got_stat[group, chip] = chip_stat[group, chip]
+            got_ctx[chip, slot, :] = chip_ctx[block(chip), :]
 
     def merge_chips(group):
+        pl.when(is_middle)(functools.partial(own_rows, group))
+
+    def own_rows(group):
         first_pair, count = groups[group]
         mode = SHARES[group]
-        sources = levels if SUMS[group] == "near" else chips
-        part_rows, block, slot = slices(first_pair, count)
-        await_copy(got_stat.at[group, pl.ds(0, sources - 1)], got_sem.at[0, group])
-        await_copy(got_ctx.at[pl.ds(0, sources - 1), pl.ds(0, part_rows)], got_sem.at[1, group])
-        stats = [got_stat[group, source] for source in range(sources)]
+        part_rows, _, block, slot = slices(first_pair, count)
+        await_copy(got_stat.at[group, pl.ds(0, chips - 1)], got_sem.at[0, group])
+        await_copy(got_ctx.at[pl.ds(0, chips - 1), pl.ds(0, part_rows)], got_sem.at[1, group])
+        stats = [got_stat[group, source] for source in range(chips)]
         top = stats[0][0:1]
         for stat in stats[1:]:
             top = jnp.maximum(top, stat[0:1])
@@ -882,11 +832,26 @@
         first_pair, count = groups[group]
         return slice(first_pair * lanes, (first_pair + count) * lanes)
 
+    def await_middle(ref, unit, amount, sem):
+        @pl.when(is_middle)
+        def _():
+            await_copy(ref.at[pl.ds(0, unit * (amount - 1))], sem)
+
+        @pl.when(jnp.logical_not(is_middle))
+        def _():
+            await_copy(ref.at[pl.ds(0, unit * amount)], sem)
+
     def await_slices(group, amount):
-        await_copy(fin_ref.at[0, pl.ds(0, amount * groups[group][1] * lanes // chips)], fin_sem.at[group])
+        unit = groups[group][1] * lanes // len(owners)
+        await_middle(fin_ref.at[0], unit, amount, fin_sem.at[group])
+
+    def side_rows(group, which):
+        first_pair, count = groups[group]
+        span = count * lanes // 2
+        return pl.ds(pl.multiple_of(first_pair * lanes + which * span, 16), span)
 
     def cross(group):
-        await_slices(group, levels - 1)
+        await_slices(group, levels // 2)
         block = fin_ref.at[core, side_rows(group, side)]
         remote(block, block, send_sem.at[9], side_sem.at[group], me + 2 - 4 * side).start()
 
@@ -894,7 +859,7 @@
         if SHARES[group] == "column":
             await_copy(fin_ref.at[0, pl.ds(0, groups[group][1] * lanes // 2)], side_sem.at[group])
         else:
-            await_slices(group, chips - 1)
+            await_slices(group, len(owners))
         block = fin_ref.at[core, group_rows(group)]
         remote(block, block, send_sem.at[8], both_sem.at[group], partner).start()
 
@@ -907,7 +872,6 @@
         "Y": await_queries,
         "A": attend,
         "M": merge_cores,
-        "S": merge_sides,
         "C": merge_chips,
         "X": cross,
         "R": relay,
@@ -930,37 +894,39 @@
     late_row = groups[direct[0]][0] * lanes
     total = attended(0, late_row)
     for group in direct:
-        await_slices(group, n - 1)
+        await_slices(group, 2 * len(owners))
     total = total + attended(late_row, width)
     total = total.astype(jnp.bfloat16)
     for step in range(steps):
         out_ref[step] = total[:, step * per_step : (step + 1) * per_step]
 
     def sent(amount, sem):
-        await_copy(fin_ref.at[0, pl.ds(0, amount)], send_sem.at[sem])
+        await_copy(q_ref.at[pl.ds(0, amount // 2)], send_sem.at[sem])
 
     share_rows = {mode: 0 for mode in SHARES}
-    sum_rows = {mode: 0 for mode in SUMS}
-    sum_count = {mode: 0 for mode in SUMS}
-    for (_, count), shared, summed in zip(groups, SHARES, SUMS):
-        share_rows[shared] += count * lanes // chips
-        sum_rows[summed] += count * lanes // chips
-        sum_count[summed] += 1
+    for (_, count), shared in zip(groups, SHARES):
+        share_rows[shared] += count * lanes // len(owners)
     await_copy(q_ref.at[pl.ds(0, rows * (chips - 1))], send_sem.at[0])
     await_copy(q_ref.at[pl.ds(0, rows * chips)], send_sem.at[1])
     await_copy(stat_ref.at[0], send_sem.at[2])
     await_copy(ctx_ref.at[0], send_sem.at[3])
-    await_copy(got_stat.at[pl.ds(0, sum_count["far"]), pl.ds(0, chips - 1)], send_sem.at[4])
-    sent((chips - 1) * sum_rows["far"], 5)
-    sent((levels - 1) * share_rows["column"] + (chips - 1) * share_rows["relay"], 6)
-    sent((n - 1) * share_rows["direct"], 7)
+    @pl.when(is_middle)
+    def _():
+        await_copy(chip_stat.at[:, pl.ds(0, len(owners) - 1)], send_sem.at[4])
+
+    @pl.when(jnp.logical_not(is_middle))
+    def _():
+        await_copy(chip_stat.at[:, pl.ds(0, len(owners))], send_sem.at[4])
+
+    await_middle(fin_ref.at[0], width // len(owners), len(owners), send_sem.at[5])
+
+    @pl.when(is_middle)
+    def _():
+        sent((levels - 1) * share_rows["column"] + (chips - 1) * share_rows["relay"], 6)
+        sent((n - 1) * share_rows["direct"], 7)
+
     sent(late_row, 8)
-    sent(levels * share_rows["column"], 9)
-    if "near" in SUMS:
-        sent((levels - 1) * sum_rows["near"], 10)
-        sent(levels * sum_rows["near"], 11)
-        await_copy(side_stat.at[pl.ds(0, sum_count["near"])], send_sem.at[12])
-        await_copy(got_stat.at[pl.ds(0, sum_count["near"]), pl.ds(0, levels - 1)], send_sem.at[13])
+    sent(share_rows["column"] * len(owners) // 2, 9)
 
 
 def paired_local(n, frames, dec_states, w_query, w_keyval, w_output, head_slope, lengths, positions):
@@ -1001,19 +967,15 @@
             pltpu.VMEM((groups, 8, per_step), jnp.float32),
             pltpu.VMEM((width, per_step), jnp.bfloat16),
             pltpu.VMEM((groups, chips, 2, per_step), jnp.float32),
-            pltpu.VMEM((chips, width // chips, per_step), jnp.bfloat16),
+            pltpu.VMEM((chips, 2 * width // chips, per_step), jnp.bfloat16),
             pltpu.VMEM((groups, chips, 2, per_step), jnp.float32),
-            pltpu.VMEM((groups, 8, per_step), jnp.float32),
-            pltpu.VMEM((groups, 8, per_step), jnp.float32),
-            pltpu.VMEM((width, per_step), jnp.bfloat16),
             pltpu.VMEM((2, width, per_step), jnp.bfloat16),
             pltpu.SemaphoreType.DMA((6,)),
             pltpu.SemaphoreType.DMA((steps,)),
             pltpu.SemaphoreType.DMA((2 * width // part,)),
-            pltpu.SemaphoreType.DMA((14,)),
+            pltpu.SemaphoreType.DMA((10,)),
             pltpu.SemaphoreType.DMA((chips,)),
             pltpu.SemaphoreType.DMA((2,)),
-            pltpu.SemaphoreType.DMA((2, groups)),
             pltpu.SemaphoreType.DMA((2, groups)),
             pltpu.SemaphoreType.DMA((2, groups)),
             pltpu.SemaphoreType.DMA((groups,)),
@@ -1051,7 +1013,7 @@
         and n % 4 == 0
         and heads % 4 == 0
         and heads // 2 == sum(count for _, count in GROUPS)
-        and n % 8 == 0
+        and n % 16 == 0
         and size == 64
         and per_step == 2 * size
         and frame_count % 128 == 0

time: 38.7 us -> 37.9 us (0.979)
  Pallas kernels: 37.9 us -> 37.1 us
    pallas_call x1, Pallas kernels: 37.9 us -> 37.1 us  [paired_local(): pl.pallas_call(functools.partial(paired_kernel, n), out_shape=pltpu.VMEM(...]
where the time goes in v3:
time: 37.9 us; the launch traced here: 37.8 us
  Pallas kernels  37.1 us (98%)
  local copies, waits for them, and re-layouts  0.62 us (2%)
    pallas_call x1, Pallas kernels, paired_local(): pl.pallas_call(functools.partial(paired_kernel, n), out_shape=pltpu.VMEM(...  37.1 us

profile of v3, /device:TPU:1, one launch (start us, length us, event | category | flops | bytes accessed | tf_op | source)
XLA Modules:
  0.0 37.8 jit_solution(12210958980708734683)
XLA Ops:
  0.0 37.1 %shard_map.82 = bf16[2,80,128]{2,1,0:T(8,128)(2,1)S(1)} custom-call(s32[1,256]{1,0:T(1,128)} %bitcast.9, f32[20]{0:T(128)} %slope_hbm.1, s32[2,16]{1,0:T(2,128)} %len_hbm.1, bf16[256,1280]{1,0:T(8,128)(2,1)} %bitcast.6, bf16[80,1280]{1,0:T(8,128)(2,1)} %bitcast.7, bf16[80,1280]{1,0:T(8,128)(2,1)} %bitcast.8, bf16[2,640,1280]{2,1,0:T(8,128)(2,1)} %frames_hbm.1, ...), custom_call_target="tpu_custom_call" | custom-call | tf_op jit(solution)/shard_map/pallas_call | solution.py:946
  37.2 0.6 %copy.10 = bf16[2,128,80]{1,2,0:T(8,128)(2,1)} copy(bf16[2,128,80]{1,2,0:T(8,128)(2,1)S(1)} %bitcast.5) | data formatting | bytes 81920

commit v4 on v3

--- a/solution.py
+++ b/solution.py
@@ -485,6 +485,7 @@
     part_pairs = half // lanes
     scale = 1.0 / math.sqrt(size)
     groups = GROUPS
+    stat_rows = 16
     side, levels = lax.rem(chip, 2), chips // 2
     owners = list(range(chips // 4, chips - chips // 4))
 
@@ -729,10 +730,10 @@
         block = pl.ds(pl.multiple_of(first_pair * lanes, lanes), count * lanes)
         other = 1 - core
         remote(
-            stat_ref.at[other, group], pair_stat.at[group], send_sem.at[2], pair_sem.at[0, group], partner
+            stat_ref.at[other, group], pair_stat.at[group], send_sem.at[2], pair_sem.at[group], partner
         ).start()
         remote(
-            ctx_ref.at[other, block], pair_ctx.at[block], send_sem.at[3], pair_sem.at[1, group], partner
+            ctx_ref.at[other, block], pair_ctx.at[block], send_sem.at[3], pair_sem.at[group], partner
         ).start()
 
     def slices(first_pair, count):
@@ -758,8 +759,7 @@
         first_pair, count = groups[group]
         part_rows, place, block, slot = slices(first_pair, count)
         heads = 2 * count
-        await_copy(pair_stat.at[group], pair_sem.at[0, group])
-        await_copy(pair_ctx.at[pl.ds(0, count * lanes)], pair_sem.at[1, group])
+        await_copy(pair_ctx.at[pl.ds(0, count * lanes + stat_rows)], pair_sem.at[group])
         top, total, one_factor, two_factor = mix(stat_ref[core, group], pair_stat[group], heads)
         for head in range(heads):
             at = slice(first_pair * lanes + head * size, first_pair * lanes + (head + 1) * size)
@@ -779,11 +779,11 @@
                     chip_stat.at[group, owner],
                     got_stat.at[group, chip],
                     send_sem.at[4],
-                    got_sem.at[0, group],
+                    got_sem.at[group],
                     peer,
                 ).start()
                 remote(
-                    chip_ctx.at[block(owner)], got_ctx.at[chip, slot], send_sem.at[5], got_sem.at[1, group], peer
+                    chip_ctx.at[block(owner)], got_ctx.at[chip, slot], send_sem.at[5], got_sem.at[group], peer
                 ).start()
 
         @pl.when(is_middle)
@@ -798,8 +798,8 @@
         first_pair, count = groups[group]
         mode = SHARES[group]
         part_rows, _, block, slot = slices(first_pair, count)
-        await_copy(got_stat.at[group, pl.ds(0, chips - 1)], got_sem.at[0, group])
-        await_copy(got_ctx.at[pl.ds(0, chips - 1), pl.ds(0, part_rows)], got_sem.at[1, group])
+        each = part_rows + stat_rows // 4
+        await_copy(fin_ref.at[0, pl.ds(0, (chips - 1) * each)], got_sem.at[group])
         stats = [got_stat[group, source] for source in range(chips)]
         top = stats[0][0:1]
         for stat in stats[1:]:
@@ -813,20 +813,17 @@
             context = part_context if context is None else context + part_context
         fin_ref[core, block(chip), :] = (context / total).astype(jnp.bfloat16)
         own = fin_ref.at[core, block(chip)]
-        if mode == "direct":
-
-            @pl.loop(1, n)
-            def _(step):
-                remote(own, own, send_sem.at[7], fin_sem.at[group], lax.rem(me + step, n)).start()
-
-        else:
-            stride = 4 if mode == "column" else 2
-
-            @pl.loop(1, n // stride)
-            def _(step):
-                remote(
-                    own, own, send_sem.at[6], fin_sem.at[group], lax.rem(me + stride * step, n)
-                ).start()
+        stride = {"direct": 1, "relay": 2, "column": 4}[mode]
+        sem = 7 if mode == "direct" else 6
+        offset = lax.rem(me, stride)
+
+        @pl.loop(0, n // stride)
+        def _(step):
+            peer = stride * step + offset
+
+            @pl.when(peer != me)
+            def _():
+                remote(own, own, send_sem.at[sem], fin_sem.at[group], peer).start()
 
     def group_rows(group):
         first_pair, count = groups[group]
@@ -976,8 +973,8 @@
             pltpu.SemaphoreType.DMA((10,)),
             pltpu.SemaphoreType.DMA((chips,)),
             pltpu.SemaphoreType.DMA((2,)),
-            pltpu.SemaphoreType.DMA((2, groups)),
-            pltpu.SemaphoreType.DMA((2, groups)),
+            pltpu.SemaphoreType.DMA((groups,)),
+            pltpu.SemaphoreType.DMA((groups,)),
             pltpu.SemaphoreType.DMA((groups,)),
             pltpu.SemaphoreType.DMA((groups,)),
             pltpu.SemaphoreType.DMA((groups,)),

time: 37.9 us -> 37.8 us (level)
  no operation moved by 1% of the time
where the time goes in v4:
time: 37.8 us; the launch traced here: 37.6 us
  Pallas kernels  37 us (98%)
  local copies, waits for them, and re-layouts  0.62 us (2%)
    pallas_call x1, Pallas kernels, paired_local(): pl.pallas_call(functools.partial(paired_kernel, n), out_shape=pltpu.VMEM(...  37 us

profile of v4, /device:TPU:1, one launch (start us, length us, event | category | flops | bytes accessed | tf_op | source)
XLA Modules:
  0.0 37.6 jit_solution(2923460220000052082)
XLA Ops:
  0.0 37.0 %shard_map.82 = bf16[2,80,128]{2,1,0:T(8,128)(2,1)S(1)} custom-call(s32[1,256]{1,0:T(1,128)} %bitcast.9, f32[20]{0:T(128)} %slope_hbm.1, s32[2,16]{1,0:T(2,128)} %len_hbm.1, bf16[256,1280]{1,0:T(8,128)(2,1)} %bitcast.6, bf16[80,1280]{1,0:T(8,128)(2,1)} %bitcast.7, bf16[80,1280]{1,0:T(8,128)(2,1)} %bitcast.8, bf16[2,640,1280]{2,1,0:T(8,128)(2,1)} %frames_hbm.1, ...), custom_call_target="tpu_custom_call" | custom-call | tf_op jit(solution)/shard_map/pallas_call | solution.py:943
  37.0 0.6 %copy.10 = bf16[2,128,80]{1,2,0:T(8,128)(2,1)} copy(bf16[2,128,80]{1,2,0:T(8,128)(2,1)S(1)} %bitcast.5) | data formatting | bytes 81920

commit v5 on v4

--- a/solution.py
+++ b/solution.py
@@ -772,18 +772,21 @@
             head = place(owner) * part_rows // size
             chip_stat[group, owner] = jnp.concatenate([top[head : head + 1], total[head : head + 1]], axis=0)
 
+        for first_owner in owners:
+            owner = jnp.where(chip < levels, chips - 1 - first_owner, first_owner)
+            rows_at = jnp.where(
+                chip < levels, place(chips - 1 - first_owner) * part_rows, place(first_owner) * part_rows
+            )
+            sent_block = pl.ds(pl.multiple_of(first_pair * lanes + rows_at, 16), part_rows)
+
             @pl.when(owner != chip)
             def _():
                 peer = 2 * owner + core
                 remote(
-                    chip_stat.at[group, owner],
-                    got_stat.at[group, chip],
-                    send_sem.at[4],
-                    got_sem.at[group],
-                    peer,
+                    chip_stat.at[group, owner], got_stat.at[group, chip], send_sem.at[4], got_sem.at[group], peer
                 ).start()
                 remote(
-                    chip_ctx.at[block(owner)], got_ctx.at[chip, slot], send_sem.at[5], got_sem.at[group], peer
+                    chip_ctx.at[sent_block], got_ctx.at[chip, slot], send_sem.at[5], got_sem.at[group], peer
                 ).start()
 
         @pl.when(is_middle)

time: 37.8 us -> 37.6 us (level)
  no operation moved by 1% of the time
where the time goes in v5:
time: 37.6 us; the launch traced here: 37.5 us
  Pallas kernels  36.8 us (98%)
  local copies, waits for them, and re-layouts  0.62 us (2%)
    pallas_call x1, Pallas kernels, paired_local(): pl.pallas_call(functools.partial(paired_kernel, n), out_shape=pltpu.VMEM(...  36.8 us

profile of v5, /device:TPU:1, one launch (start us, length us, event | category | flops | bytes accessed | tf_op | source)
XLA Modules:
  0.0 37.5 jit_solution(14418297979592330685)
XLA Ops:
  0.0 36.8 %shard_map.82 = bf16[2,80,128]{2,1,0:T(8,128)(2,1)S(1)} custom-call(s32[1,256]{1,0:T(1,128)} %bitcast.9, f32[20]{0:T(128)} %slope_hbm.1, s32[2,16]{1,0:T(2,128)} %len_hbm.1, bf16[256,1280]{1,0:T(8,128)(2,1)} %bitcast.6, bf16[80,1280]{1,0:T(8,128)(2,1)} %bitcast.7, bf16[80,1280]{1,0:T(8,128)(2,1)} %bitcast.8, bf16[2,640,1280]{2,1,0:T(8,128)(2,1)} %frames_hbm.1, ...), custom_call_target="tpu_custom_call" | custom-call | tf_op jit(solution)/shard_map/pallas_call | solution.py:946
  36.9 0.6 %copy.10 = bf16[2,128,80]{1,2,0:T(8,128)(2,1)} copy(bf16[2,128,80]{1,2,0:T(8,128)(2,1)S(1)} %bitcast.5) | data formatting | bytes 81920
